TPU v7x, 32 devices: a whole 2x2x4 slice. The times are simulated.
32 devices in a mesh: ma: 2 (over y), an: 4 (over z), ka: 4 (over x, core).
Axes of the slice: x: 2, y: 2, z: 4, core: 2. Of those that a mesh axis runs over, the one named last changes fastest.
Arguments:
- left_matrix: float32 [16384, 2048], P(('ka', 'an'), 'ma'), may hold values from -6 to 6
- right_matrix: float32 [16384, 3072], P(('ka', 'ma'), 'an'), may hold values from -0.046875 to 0.046875
Outputs:
- product: float32 [2048, 3072], P(('ma', 'ka'), 'an')
All inputs are finite; a program needn't handle non-finite values.
Results may differ from a plain program's by a relative error of at most 0.000098.
Values sent between devices are 32-bit elements; how exact they have to be, the bound alone decides.
A program may use at most 128 MiB of HBM per device.

v0:
```python
import jax
import jax.numpy as jnp
from jax import lax
from jax.sharding import PartitionSpec as P


def multiply(left_part, right_part):
    return lax.dot_general(
        left_part,
        right_part,
        (((0,), (0,)), ((), ())),
        precision=lax.Precision.HIGHEST,
        preferred_element_type=jnp.float32,
    )


def per_device(left_matrix, right_matrix):
    b_block = lax.all_gather(right_matrix, "ma", axis=0, tiled=True)
    a_block = lax.all_gather(left_matrix, "an", axis=0, tiled=True)
    partial_value = multiply(a_block, b_block)
    summed = lax.psum_scatter(partial_value, "ka", scatter_dimension=0, tiled=True)
    return summed


def solution(mesh):
    placed = (P(("ka", "an"), "ma"), P(("ka", "ma"), "an"))
    return jax.shard_map(
        per_device, mesh=mesh, in_specs=placed, out_specs=P(("ma", "ka"), "an"), check_vma=False
    )
```

profile of v0, /device:TPU:8, one launch (start us, length us, event | category | flops | bytes accessed | tf_op | source)
XLA Modules:
  0.0 540.4 jit_solution(16185840921908149508)
XLA Ops:
  6.5 0.0 all-gather.5.cloned.1.call-start
  6.5 0.7 all-gather.5.cloned.1.call-update
  7.3 0.0 all-gather.3.cloned.1.call-start
  7.3 0.7 all-gather.3.cloned.1.call-update
  8.0 0.0 reduce-scatter.2.cloned.1.call-start
  8.1 154.5 %all-gather.5.cloned.1.call-done = f32[4096,768]{1,0:T(8,128)} async-done(((f32[2048,768]{1,0:T(8,128)}), f32[4096,768]{1,0:T(8,128)}) %all-gather.5.cloned.1.call-update) | async-done | bytes 12582928 | tf_op jit(solution)/shard_map/all_gather | solution.py:18
  162.6 285.4 %all-gather.3.cloned.1.call-done = f32[4096,1024]{1,0:T(8,128)} async-done(((f32[1024,1024]{1,0:T(8,128)}), f32[4096,1024]{1,0:T(8,128)}) %all-gather.3.cloned.1.call-update) | async-done | bytes 16777232 | tf_op jit(solution)/shard_map/all_gather | solution.py:19
  448.0 46.7 %fusion = f32[1024,768]{1,0:T(8,128)} fusion(f32[4096,1024]{1,0:T(8,128)} %all-gather.3.cloned.1.call-done, f32[4096,768]{1,0:T(8,128)} %all-gather.5.cloned.1.call-done), kind=kOutput, calls=%fused_computation | convolution fusion | flops 38654705664 | bytes 32505856 | tf_op jit(solution)/shard_map/dot_general | solution.py:8
  494.7 0.0 reduce-scatter.2.cloned.1.call-update
  494.7 39.2 %reduce-scatter.2.cloned.1.call-done = f32[256,768]{1,0:T(8,128)} async-done(((f32[1024,768]{1,0:T(8,128)}), f32[256,768]{1,0:T(8,128)}) %reduce-scatter.2.cloned.1.call-update) | async-done | bytes 786448 | tf_op jit(solution)/shard_map/reduce_scatter | solution.py:21
Async XLA Ops:
  6.5 156.0 %all-gather.5.cloned.1.call-start = ((), (), s32[]{:S(2)}) async-start(), calls=%async_computation.2 | async-start | bytes 18874368 | tf_op jit(solution)/shard_map/all_gather | solution.py:18
  7.3 440.7 %all-gather.3.cloned.1.call-start = ((), (), s32[]{:S(2)}) async-start(), calls=%async_computation.1 | async-start | bytes 20971520 | tf_op jit(solution)/shard_map/all_gather | solution.py:19
  8.0 525.9 %reduce-scatter.2.cloned.1.call-start = ((), (), s32[]{:S(2)}) async-start(), calls=%async_computation.3 | async-start | bytes 3932160 | tf_op jit(solution)/shard_map/reduce_scatter | solution.py:21
Sparse Core Ops, SparseCore 0:
  8.9 153.6 all-gather.4
  164.1 283.7 all-gather.2
  494.9 39.0 reduce-scatter.1
where the time goes:
time: 542 us; the launch traced here: 540 us
  waiting for transfers between devices  481 us (89%)
  matrix products  46.7 us (9%)
  between operations  13.1 us (2%)
    all_gather x1, waiting for transfers between devices, per_device(): a_block = lax.all_gather(left_matrix, 'an', axis=0, tiled=True)  285 us
    all_gather x1, waiting for transfers between devices, per_device(): b_block = lax.all_gather(right_matrix, 'ma', axis=0, tiled=True)  155 us
    dot_general x1, matrix products, multiply(): lax.dot_general(left_part, right_part, (((0,), (0,)), ((), ())), precisio...  46.7 us
    reduce_scatter x1, waiting for transfers between devices, per_device(): lax.psum_scatter(partial_value, 'ka', scatter_dimension=0, tiled=True)  39.2 us
  transfers between devices with their start and end apart: 3, of which 3 were waited for; matrix products, arithmetic and copies ran while one was open for 0% of the time, Pallas kernels for 0%

commit v1 on v0

v1 whole, which is shorter than its diff:
```python
import functools

import jax
import jax.numpy as jnp
from jax import lax
from jax.experimental import pallas as pl
from jax.experimental.pallas import tpu as pltpu
from jax.sharding import PartitionSpec as P

MESH = pl.DeviceIdType.MESH
PIECES = 4


def multiply(left_part, right_part):
    return lax.dot_general(
        left_part,
        right_part,
        (((0,), (0,)), ((), ())),
        precision=lax.Precision.HIGHEST,
        preferred_element_type=jnp.float32,
    )


def gather_both(left_matrix, right_matrix):
    b_block = lax.all_gather(right_matrix, "ma", axis=0, tiled=True)
    a_block = lax.all_gather(left_matrix, "an", axis=0, tiled=True)
    partial_value = multiply(a_block, b_block)
    return lax.psum_scatter(partial_value, "ka", scatter_dimension=0, tiled=True)


def halves(value):
    high = value.astype(jnp.bfloat16)
    low = (value - high.astype(jnp.float32)).astype(jnp.bfloat16)
    return high, low


def kernel(
    a_hbm, b_hbm, out,
    a_own, a_got, at_hi, at_lo, passing, b_got, b_hi, b_lo,
    part, core_got, x_got, z_got, y_sum, y_got,
    a_local, a_send, a_recv, pass_send, pass_recv, b_send, b_recv,
    core_send, core_recv, x_send, x_recv, z_send, z_recv, y_sem,
):
    ma, an, ka = lax.axis_index("ma"), lax.axis_index("an"), lax.axis_index("ka")
    x, core = ka // 2, lax.rem(ka, 2)
    other_y = 1 - ma
    over_core = x * 2 + (1 - core)
    over_x = (1 - x) * 2 + core
    depth, width = a_hbm.shape[0], b_got.shape[-1]
    rows = depth // PIECES
    band = a_own.shape[-1]

    def differs(one, two):
        return lax.rem(one // 2 + two // 2, 2) * 2 + lax.rem(one + two, 2)

    def at_distance(step):
        return lax.rem(an // 2 + step // 2, 2) * 2 + lax.rem(an + step, 2)

    def remote(source, target, send, recv, **where):
        return pltpu.make_async_remote_copy(
            src_ref=source, dst_ref=target, send_sem=send, recv_sem=recv,
            device_id=where, device_id_type=MESH,
        )

    barrier = pltpu.get_barrier_semaphore()
    peers = [{"ma": other_y}, {"ka": over_core}, {"ka": over_x}]
    peers += [{"an": at_distance(step)} for step in range(1, 4)]
    for peer in peers:
        pl.semaphore_signal(barrier, inc=1, device_id=peer, device_id_type=MESH)
    pl.semaphore_wait(barrier, len(peers))

    keep = pl.multiple_of(ma * width, 128)
    give = pl.multiple_of(other_y * width, 128)

    def pass_copy(which, piece):
        return remote(
            b_hbm.at[pl.ds(which * depth + piece * rows, rows), pl.ds(give, width)],
            passing.at[which, piece],
            pass_send.at[which, piece], pass_recv.at[which, piece], ma=other_y,
        )

    def a_copy(block):
        return remote(
            a_hbm.at[:, pl.ds(block * band, band)], a_got.at[block],
            a_send.at[block], a_recv.at[block], ma=other_y,
        )

    def own_copy(block):
        return pltpu.make_async_copy(
            a_hbm.at[:, pl.ds(block * band, band)], a_own.at[block], a_local.at[block]
        )

    def place(kind, which, piece):
        goal = (ma if kind == 0 else other_y) * 2 + which
        slot = differs(an, goal)
        if kind == 0:
            source = b_hbm.at[pl.ds(which * depth + piece * rows, rows), pl.ds(keep, width)]
        else:
            source = passing.at[which, piece]
        target = b_got.at[slot, piece]
        far = remote(
            source, target, b_send.at[kind, which, piece], b_recv.at[slot, piece], an=goal
        )
        near = pltpu.make_async_copy(source, target, b_recv.at[slot, piece])
        return goal, far, near

    def start_place(kind, which, piece):
        goal, far, near = place(kind, which, piece)

        @pl.when(goal != an)
        def _():
            far.start()

        @pl.when(goal == an)
        def _():
            near.start()

    for piece in range(PIECES):
        for which in range(2):
            pass_copy(which, piece).start()
            start_place(0, which, piece)
    for block in range(4):
        own_copy(block).start()
        a_copy(block).start()

    def turn(side, source, block):
        for cut in range(PIECES):
            span = pl.ds(cut * rows, rows)
            high, low = halves(source[block, span, :].T)
            at_hi[side, block, :, span] = high
            at_lo[side, block, :, span] = low

    for piece in range(PIECES):
        for which in range(2):
            pass_copy(which, piece).wait_recv()
            start_place(1, which, piece)
        own_copy(piece).wait()
        turn(0, a_own, piece)

    def b_wait(step):
        for piece in range(PIECES):
            pltpu.make_async_copy(
                passing.at[0, 0], b_got.at[step, piece], b_recv.at[step, piece]
            ).wait()

    def core_copy(unit, xo):
        return remote(
            part.at[unit, xo * 2 + (1 - core)], core_got.at[unit, xo],
            core_send.at[unit, xo], core_recv.at[unit, xo], ka=over_core,
        )

    def x_copy(unit):
        return remote(
            part.at[unit, over_x], x_got.at[unit], x_send.at[unit], x_recv.at[unit], ka=over_x
        )

    def z_copy(unit):
        side, step = unit // 4, unit % 4
        return remote(
            part.at[unit, ka], z_got.at[side, step - 1],
            z_send.at[unit], z_recv.at[side, step - 1], an=at_distance(step),
        )

    def compute(unit):
        side, step = unit // 4, unit % 4
        if side == 0:
            b_wait(step)
            for piece in range(PIECES):
                high, low = halves(b_got[step, piece])
                b_hi[step, pl.ds(piece * rows, rows), :] = high
                b_lo[step, pl.ds(piece * rows, rows), :] = low

        @pl.loop(0, 4)
        def _(block):
            dot = functools.partial(jnp.dot, preferred_element_type=jnp.float32)
            part[unit, block] = (
                dot(at_hi[side, block], b_lo[step]) + dot(at_lo[side, block], b_hi[step])
            ) + dot(at_hi[side, block], b_hi[step])

        for xo in range(2):
            core_copy(unit, xo).start()

    def add_core(unit):
        for xo in range(2):
            core_copy(unit, xo).wait_recv()
            part[unit, xo * 2 + core] += core_got[unit, xo]
        x_copy(unit).start()

    def add_x(unit):
        x_copy(unit).wait_recv()
        part[unit, ka] += x_got[unit]
        if unit % 4:
            z_copy(unit).start()

    def total(side):
        value = part[side * 4, ka]
        for step in range(1, 4):
            z_copy(side * 4 + step).wait_recv()
            value = value + z_got[side, step - 1]
        return value

    for unit in range(8):
        if unit == 4:
            for block in range(4):
                a_copy(block).wait_recv()
                turn(1, a_got, block)
        compute(unit)
        if unit >= 1:
            add_core(unit - 1)
        if unit >= 2:
            add_x(unit - 2)
    add_core(7)
    add_x(6)
    add_x(7)

    y_copy = remote(y_sum, y_got, y_sem.at[0], y_sem.at[1], ma=other_y)
    y_sum[...] = total(1)
    y_copy.start()
    out[:, pl.ds(keep, width)] = total(0)
    y_copy.wait_recv()
    out[:, pl.ds(give, width)] = y_got[...]

    y_copy.wait_send()
    for piece in range(PIECES):
        for which in range(2):
            pass_copy(which, piece).wait_send()
            for kind in range(2):
                goal, far, _ = place(kind, which, piece)

                @pl.when(goal != an)
                def _():
                    far.wait_send()

    for block in range(4):
        a_copy(block).wait_send()
    for unit in range(8):
        for xo in range(2):
            core_copy(unit, xo).wait_send()
        x_copy(unit).wait_send()
        if unit % 4:
            z_copy(unit).wait_send()


def exchange(left_matrix, right_matrix):
    depth, tall = left_matrix.shape
    width = right_matrix.shape[1] // 2
    band, rows = tall // 4, depth // PIECES
    f32, bf16, dma = jnp.float32, jnp.bfloat16, pltpu.SemaphoreType.DMA
    return pl.pallas_call(
        kernel,
        out_shape=jax.ShapeDtypeStruct((band, 2 * width), f32),
        in_specs=[pl.BlockSpec(memory_space=pl.ANY)] * 2,
        out_specs=pl.BlockSpec(memory_space=pltpu.VMEM),
        scratch_shapes=[
            pltpu.VMEM((4, depth, band), f32),
            pltpu.VMEM((4, depth, band), f32),
            pltpu.VMEM((2, 4, band, depth), bf16),
            pltpu.VMEM((2, 4, band, depth), bf16),
            pltpu.VMEM((2, PIECES, rows, width), f32),
            pltpu.VMEM((4, PIECES, rows, width), f32),
            pltpu.VMEM((4, depth, width), bf16),
            pltpu.VMEM((4, depth, width), bf16),
            pltpu.VMEM((8, 4, band, width), f32),
            pltpu.VMEM((8, 2, band, width), f32),
            pltpu.VMEM((8, band, width), f32),
            pltpu.VMEM((2, 3, band, width), f32),
            pltpu.VMEM((band, width), f32),
            pltpu.VMEM((band, width), f32),
            dma((4,)), dma((4,)), dma((4,)),
            dma((2, PIECES)), dma((2, PIECES)),
            dma((2, 2, PIECES)), dma((4, PIECES)),
            dma((8, 2)), dma((8, 2)), dma((8,)), dma((8,)),
            dma((8,)), dma((2, 3)), dma((2,)),
        ],
        compiler_params=pltpu.CompilerParams(
            collective_id=0, has_side_effects=True, vmem_limit_bytes=67043328
        ),
    )(left_matrix, right_matrix)


def fits(mesh, left, right):
    sizes = (mesh.shape["ma"], mesh.shape["an"], mesh.shape["ka"])
    if sizes != (2, 4, 4):
        return False
    depth, tall, width = left[0] // 16, left[1] // 2, right[1] // 8
    aligned = depth % 512 == 0 and tall % 512 == 0 and width % 128 == 0
    need = 4 * (3 * depth * tall + 9 * depth * width + 17 * tall * width)
    return aligned and need < 63 * 2**20


def solution(mesh):
    placed = (P(("ka", "an"), "ma"), P(("ka", "ma"), "an"))

    def run(left_matrix, right_matrix):
        body = exchange if fits(mesh, left_matrix.shape, right_matrix.shape) else gather_both
        return jax.shard_map(
            body, mesh=mesh, in_specs=placed, out_specs=P(("ma", "ka"), "an"), check_vma=False
        )(left_matrix, right_matrix)

    return run
```

time: 542 us -> 248 us (0.46)
  waiting for transfers between devices: 481 us -> 0 us
  Pallas kernels: 0 us -> 246 us
  matrix products: 46.7 us -> 0 us
  between operations: 13.1 us -> 0.01 us
    all_gather x2 -> x0, waiting for transfers between devices: 440 us -> none  [the longest x1 285 us: per_device(): a_block = lax.all_gather(left_matrix, 'an', axis=0, tiled=True)]
    pallas_call x0 -> x1, Pallas kernels: none -> 246 us  [exchange(): pl.pallas_call(kernel, out_shape=jax.ShapeDtypeStruct((band, 2 * width),...]
    dot_general x1 -> x0, matrix products: 46.7 us -> none  [multiply(): lax.dot_general(left_part, right_part, (((0,), (0,)), ((), ())), precisio...]
    reduce_scatter x1 -> x0, waiting for transfers between devices: 39.2 us -> none  [per_device(): lax.psum_scatter(partial_value, 'ka', scatter_dimension=0, tiled=True)]
  transfers between devices with their start and end apart: 3 -> 0, of which waited for: 3 -> 0; matrix products, arithmetic and copies ran while one was open for 0% -> 0% of each run, Pallas kernels for 0% -> 0%
where the time goes in v1:
time: 248 us
  Pallas kernels  246 us (99%)
    pallas_call x1, Pallas kernels, exchange(): pl.pallas_call(kernel, out_shape=jax.ShapeDtypeStruct((band, 2 * width),...  246 us

profile of v1, /device:TPU:8, one launch (start us, length us, event | category | flops | bytes accessed | tf_op | source)
XLA Modules:
  0.0 248.0 jit_solution(15648150643398146139)
XLA Ops:
  0.0 246.0 %shard_map.28 = f32[256,768]{1,0:T(8,128)} custom-call(f32[1024,1024]{1,0:T(8,128)} %a_hbm.1, f32[2048,768]{1,0:T(8,128)} %b_hbm.1), custom_call_target="tpu_custom_call" | custom-call | tf_op jit(solution)/shard_map/pallas_call | solution.py:249
  246.0 2.1 copy.4

commit v2 on v1

--- a/solution.py
+++ b/solution.py
@@ -71,18 +71,22 @@
 
     keep = pl.multiple_of(ma * width, 128)
     give = pl.multiple_of(other_y * width, 128)
-
-    def pass_copy(which, piece):
-        return remote(
-            b_hbm.at[pl.ds(which * depth + piece * rows, rows), pl.ds(give, width)],
-            passing.at[which, piece],
-            pass_send.at[which, piece], pass_recv.at[which, piece], ma=other_y,
-        )
-
-    def a_copy(block):
-        return remote(
-            a_hbm.at[:, pl.ds(block * band, band)], a_got.at[block],
-            a_send.at[block], a_recv.at[block], ma=other_y,
+    sides_x = (1 - x, x)
+    turns = [sides_x[order // 2] * 2 + lax.rem(1 - core + order, 2) for order in range(4)]
+    goals = (lax.rem(an, 2), 1 - lax.rem(an, 2))
+
+    def pass_copy(order, piece):
+        return remote(
+            b_hbm.at[pl.ds(goals[order] * depth + piece * rows, rows), pl.ds(give, width)],
+            passing.at[order, piece],
+            pass_send.at[order, piece], pass_recv.at[order, piece], ma=other_y,
+        )
+
+    def a_copy(order):
+        columns = pl.ds(pl.multiple_of(turns[order] * band, 128), band)
+        return remote(
+            a_hbm.at[:, columns], a_got.at[order],
+            a_send.at[order], a_recv.at[order], ma=other_y,
         )
 
     def own_copy(block):
@@ -90,22 +94,24 @@
             a_hbm.at[:, pl.ds(block * band, band)], a_own.at[block], a_local.at[block]
         )
 
-    def place(kind, which, piece):
-        goal = (ma if kind == 0 else other_y) * 2 + which
+    def place(kind, order, piece):
+        goal = (ma if kind == 0 else other_y) * 2 + goals[order]
         slot = differs(an, goal)
         if kind == 0:
-            source = b_hbm.at[pl.ds(which * depth + piece * rows, rows), pl.ds(keep, width)]
+            source = b_hbm.at[
+                pl.ds(goals[order] * depth + piece * rows, rows), pl.ds(keep, width)
+            ]
         else:
-            source = passing.at[which, piece]
+            source = passing.at[order, piece]
         target = b_got.at[slot, piece]
         far = remote(
-            source, target, b_send.at[kind, which, piece], b_recv.at[slot, piece], an=goal
+            source, target, b_send.at[kind, order, piece], b_recv.at[slot, piece], an=goal
         )
         near = pltpu.make_async_copy(source, target, b_recv.at[slot, piece])
         return goal, far, near
 
-    def start_place(kind, which, piece):
-        goal, far, near = place(kind, which, piece)
+    def start_place(kind, order, piece):
+        goal, far, near = place(kind, order, piece)
 
         @pl.when(goal != an)
         def _():
@@ -115,38 +121,43 @@
         def _():
             near.start()
 
-    for piece in range(PIECES):
-        for which in range(2):
-            pass_copy(which, piece).start()
-            start_place(0, which, piece)
+    for order in range(2):
+        for piece in range(PIECES):
+            pass_copy(order, piece).start()
+            start_place(0, order, piece)
     for block in range(4):
         own_copy(block).start()
         a_copy(block).start()
 
-    def turn(side, source, block):
+    def turn(side, source, held, block):
         for cut in range(PIECES):
             span = pl.ds(cut * rows, rows)
-            high, low = halves(source[block, span, :].T)
+            high, low = halves(source[held, span, :].T)
             at_hi[side, block, :, span] = high
             at_lo[side, block, :, span] = low
 
-    for piece in range(PIECES):
-        for which in range(2):
-            pass_copy(which, piece).wait_recv()
-            start_place(1, which, piece)
-        own_copy(piece).wait()
-        turn(0, a_own, piece)
+    for order in range(2):
+        for piece in range(PIECES):
+            pass_copy(order, piece).wait_recv()
+            start_place(1, order, piece)
+            if piece % 2:
+                block = order * 2 + piece // 2
+                own_copy(block).wait()
+                turn(0, a_own, block, block)
 
     def b_wait(step):
         for piece in range(PIECES):
             pltpu.make_async_copy(
                 passing.at[0, 0], b_got.at[step, piece], b_recv.at[step, piece]
             ).wait()
-
-    def core_copy(unit, xo):
-        return remote(
-            part.at[unit, xo * 2 + (1 - core)], core_got.at[unit, xo],
-            core_send.at[unit, xo], core_recv.at[unit, xo], ka=over_core,
+            high, low = halves(b_got[step, piece])
+            b_hi[step, pl.ds(piece * rows, rows), :] = high
+            b_lo[step, pl.ds(piece * rows, rows), :] = low
+
+    def core_copy(unit, near):
+        return remote(
+            part.at[unit, sides_x[near] * 2 + (1 - core)], core_got.at[unit, near],
+            core_send.at[unit, near], core_recv.at[unit, near], ka=over_core,
         )
 
     def x_copy(unit):
@@ -156,62 +167,82 @@
 
     def z_copy(unit):
         side, step = unit // 4, unit % 4
-        return remote(
-            part.at[unit, ka], z_got.at[side, step - 1],
-            z_send.at[unit], z_recv.at[side, step - 1], an=at_distance(step),
-        )
-
-    def compute(unit):
-        side, step = unit // 4, unit % 4
-        if side == 0:
-            b_wait(step)
-            for piece in range(PIECES):
-                high, low = halves(b_got[step, piece])
-                b_hi[step, pl.ds(piece * rows, rows), :] = high
-                b_lo[step, pl.ds(piece * rows, rows), :] = low
-
-        @pl.loop(0, 4)
-        def _(block):
+        slot = {1: 0, 3: 1, 2: 2}[step]
+        return remote(
+            part.at[unit, ka], z_got.at[side, slot],
+            z_send.at[side, slot], z_recv.at[side, slot], an=at_distance(2 if step == 2 else 1),
+        )
+
+    def compute(side, step, near):
+        unit = side * 4 + step
+
+        @pl.loop(0, 2)
+        def _(turned):
+            block = sides_x[near] * 2 + lax.rem(1 - core + turned, 2)
             dot = functools.partial(jnp.dot, preferred_element_type=jnp.float32)
             part[unit, block] = (
                 dot(at_hi[side, block], b_lo[step]) + dot(at_lo[side, block], b_hi[step])
             ) + dot(at_hi[side, block], b_hi[step])
 
-        for xo in range(2):
-            core_copy(unit, xo).start()
-
-    def add_core(unit):
-        for xo in range(2):
-            core_copy(unit, xo).wait_recv()
-            part[unit, xo * 2 + core] += core_got[unit, xo]
-        x_copy(unit).start()
-
-    def add_x(unit):
+        core_copy(unit, near).start()
+
+    def settle(side, step, near):
+        unit = side * 4 + step
+        core_copy(unit, near).wait_recv()
+        if not near:
+            part[unit, over_x] += core_got[unit, near]
+            x_copy(unit).start()
+            return
         x_copy(unit).wait_recv()
-        part[unit, ka] += x_got[unit]
-        if unit % 4:
+        part[unit, ka] += core_got[unit, near] + x_got[unit]
+        if step % 2:
             z_copy(unit).start()
 
+    def join_pairs(side):
+        z_copy(side * 4 + 3).wait_recv()
+        part[side * 4 + 2, ka] += z_got[side, 1]
+        z_copy(side * 4 + 2).start()
+
     def total(side):
-        value = part[side * 4, ka]
-        for step in range(1, 4):
-            z_copy(side * 4 + step).wait_recv()
-            value = value + z_got[side, step - 1]
-        return value
-
-    for unit in range(8):
-        if unit == 4:
-            for block in range(4):
-                a_copy(block).wait_recv()
-                turn(1, a_got, block)
-        compute(unit)
-        if unit >= 1:
-            add_core(unit - 1)
-        if unit >= 2:
-            add_x(unit - 2)
-    add_core(7)
-    add_x(6)
-    add_x(7)
+        z_copy(side * 4 + 1).wait_recv()
+        value = part[side * 4, ka] + z_got[side, 0]
+        z_copy(side * 4 + 2).wait_recv()
+        return value + z_got[side, 2]
+
+    def a_wait(order):
+        a_copy(order).wait_recv()
+        turn(1, a_got, order, turns[order])
+
+    waiting = []
+
+    def job(side, step, near):
+        compute(side, step, near)
+        if waiting:
+            settle(*waiting.pop())
+        waiting.append((side, step, near))
+
+    for step in range(3):
+        b_wait(step)
+        job(0, step, 0)
+        job(0, step, 1)
+    for order in range(2):
+        a_wait(order)
+    for step in range(3):
+        job(1, step, 0)
+    b_wait(3)
+    job(0, 3, 0)
+    job(1, 3, 0)
+    job(0, 3, 1)
+    settle(*waiting.pop())
+    for order in range(2, 4):
+        a_wait(order)
+    job(1, 3, 1)
+    job(1, 1, 1)
+    join_pairs(0)
+    job(1, 2, 1)
+    job(1, 0, 1)
+    join_pairs(1)
+    settle(*waiting.pop())
 
     y_copy = remote(y_sum, y_got, y_sem.at[0], y_sem.at[1], ma=other_y)
     y_sum[...] = total(1)
@@ -221,21 +252,21 @@
     out[:, pl.ds(give, width)] = y_got[...]
 
     y_copy.wait_send()
-    for piece in range(PIECES):
-        for which in range(2):
-            pass_copy(which, piece).wait_send()
+    for order in range(2):
+        for piece in range(PIECES):
+            pass_copy(order, piece).wait_send()
             for kind in range(2):
-                goal, far, _ = place(kind, which, piece)
+                goal, far, _ = place(kind, order, piece)
 
                 @pl.when(goal != an)
                 def _():
                     far.wait_send()
 
-    for block in range(4):
-        a_copy(block).wait_send()
+    for order in range(4):
+        a_copy(order).wait_send()
     for unit in range(8):
-        for xo in range(2):
-            core_copy(unit, xo).wait_send()
+        for near in range(2):
+            core_copy(unit, near).wait_send()
         x_copy(unit).wait_send()
         if unit % 4:
             z_copy(unit).wait_send()
@@ -270,7 +301,7 @@
             dma((2, PIECES)), dma((2, PIECES)),
             dma((2, 2, PIECES)), dma((4, PIECES)),
             dma((8, 2)), dma((8, 2)), dma((8,)), dma((8,)),
-            dma((8,)), dma((2, 3)), dma((2,)),
+            dma((2, 3)), dma((2, 3)), dma((2,)),
         ],
         compiler_params=pltpu.CompilerParams(
             collective_id=0, has_side_effects=True, vmem_limit_bytes=67043328

time: 248 us -> 242 us (0.976)
  Pallas kernels: 246 us -> 238 us
    pallas_call x1, Pallas kernels: 246 us -> 238 us  [exchange(): pl.pallas_call(kernel, out_shape=jax.ShapeDtypeStruct((band, 2 * width),...]
where the time goes in v2:
time: 242 us; the launch traced here: 240 us
  Pallas kernels  238 us (98%)
    pallas_call x1, Pallas kernels, exchange(): pl.pallas_call(kernel, out_shape=jax.ShapeDtypeStruct((band, 2 * width),...  238 us

profile of v2, /device:TPU:8, one launch (start us, length us, event | category | flops | bytes accessed | tf_op | source)
XLA Modules:
  0.0 240.4 jit_solution(3446659633781589581)
XLA Ops:
  0.0 238.4 %shard_map.28 = f32[256,768]{1,0:T(8,128)} custom-call(f32[1024,1024]{1,0:T(8,128)} %a_hbm.1, f32[2048,768]{1,0:T(8,128)} %b_hbm.1), custom_call_target="tpu_custom_call" | custom-call | tf_op jit(solution)/shard_map/pallas_call | solution.py:280
  238.4 2.1 copy.4
